TPU v7x, 32 devices: a whole 2x2x4 slice. The times are simulated.
32 devices in a mesh: ta: 8 (over y, x, core), sa: 4 (over z).
Axes of the slice: x: 2, y: 2, z: 4, core: 2. Of those that a mesh axis runs over, the one named last changes fastest.
Arguments:
- eigenvectors: bfloat16 [8, 256, 2, 3, 4, 384], P('ta', None, None, None, 'sa'), may hold values from -17 to 17
- momenta: int32 [8, 3], replicated, may hold values from -4 to 4
- block_order: int32 [4], replicated, may hold values from 0 to 3, each once
Outputs:
- meson_fields: float32 [8, 16, 64, 8, 128], P(None, 'sa', 'ta')
- slice_norms: float32 [8, 256], P('ta')
Inputs may be any that keep to these rules, and one draw needn't show every extreme that they name: block_order names every block once.
All inputs are finite; a program needn't handle non-finite values.
Results may differ from a plain program's by a relative error of at most 0.0018.
Values sent between devices are 32-bit elements; how exact they have to be, the bound alone decides.
A program may use at most 64 MiB of HBM per device.

v0:
```python
import math

import jax
import jax.numpy as jnp
from jax import lax
from jax.sharding import PartitionSpec as P

NC = 3
BS = 64
NBLK = 4
LX = 96


full_turn = 2.0 * math.pi


def phased_right(blocks, cos_table, sin_table):
    real_part = blocks[:, :, 0].astype(jnp.float32)[None]
    imag_part = blocks[:, :, 1].astype(jnp.float32)[None]
    cos_full = cos_table[:, None, None, None, :]
    sin_full = sin_table[:, None, None, None, :]
    phased_re = (real_part * cos_full + imag_part * sin_full).astype(jnp.bfloat16)
    phased_im = (imag_part * cos_full - real_part * sin_full).astype(jnp.bfloat16)
    first_half = jnp.stack([phased_re, phased_im], axis=3)
    second_half = jnp.stack([phased_im, -phased_re], axis=3)
    right_cols = jnp.stack([first_half, second_half], axis=1)
    return right_cols.reshape(right_cols.shape[0], 2, right_cols.shape[2], right_cols.shape[3], -1)


def spatial_norms(slab_data, plane_count, planes):
    local_sums = jnp.sum(jnp.square(slab_data.astype(jnp.float32)), axis=(2, 3, 4)).reshape(-1)
    summed = lax.psum(local_sums, "sa")
    return (summed / (2 * NC * plane_count * planes))[None, :]


def body(eigenvectors, momenta, block_order):
    planes = eigenvectors.shape[-1]
    plane_count = lax.axis_size("sa")
    slab_data = eigenvectors.reshape(NBLK, BS, 2, NC, planes)
    ordered = jnp.take(slab_data, block_order, axis=0)
    left_rows = ordered.reshape(NBLK, BS, 2 * NC * planes)
    site_index = jnp.arange(planes, dtype=jnp.int32)
    x_coord = site_index % LX
    y_coord = site_index // LX
    z_coord = lax.axis_index("sa")
    phase_index = (
        momenta[:, 0:1] * x_coord[None, :]
        + momenta[:, 1:2] * y_coord[None, :]
        + momenta[:, 2:3] * z_coord
    )
    phase_index = jnp.mod(phase_index, LX)
    angles = phase_index.astype(jnp.float32) * (full_turn / LX)
    cosines = jnp.cos(angles)
    sine_vals = jnp.sin(angles)
    norm_scale = 1.0 / math.sqrt(2 * NC * plane_count * planes)

    def one_momentum(trig_pair):
        right_cols = phased_right(ordered, trig_pair[0], trig_pair[1])[0]
        product = jnp.einsum(
            "ark,cbjk->abrcj", left_rows, right_cols, preferred_element_type=jnp.float32
        )
        return product.reshape(NBLK * NBLK, BS, 2 * BS)

    fields = lax.map(one_momentum, (cosines[:, None, :], sine_vals[:, None, :]))
    owned_sums = lax.psum_scatter(fields, "sa", scatter_dimension=1, tiled=True)
    expanded = (owned_sums * norm_scale)[:, :, :, None, :]
    meson_fields = lax.all_to_all(expanded, "ta", split_axis=2, concat_axis=3, tiled=True)
    slice_norms = spatial_norms(slab_data, plane_count, planes)
    return (meson_fields, slice_norms)


def solution(mesh):
    return jax.shard_map(
        body,
        mesh=mesh,
        in_specs=(P("ta", None, None, None, "sa", None), P(), P()),
        out_specs=(P(None, "sa", "ta", None, None), P("ta", None)),
        check_vma=False,
    )
```

profile of v0, /device:TPU:0, one launch (start us, length us, event | category | flops | bytes accessed | tf_op | source)
XLA Modules:
  0.0 381.2 jit_solution(13691788027556855198)
XLA Ops:
  17.8 174.8 %while.10 = (s32[]{:T(128)}, f32[8,16,64,128]{3,2,1,0:T(8,128)}, bf16[4,64,2,3,384]{4,3,1,0,2:T(4,128)(2,1)S(1)}, f32[8,1,384]{2,0,1:T(8,128)S(1)}, f32[8,1,384]...) while((s32[]{:T(128)}, f32[8,16,64,128]{3,2,1,0:T(8,128)}, ...), condition=%wide.region_1.2_spmd, body=%wide.region_0.1_spmd.sunk | while | flops 613711872 | bytes 29635180 | solution.py:64
  22.8 4.0 %stack.21 = bf16[1,4,64,2304]{3,2,1,0:T(8,128)(2,1)} reshape(bf16[1,4,64,2,3,384]{5,4,3,2,1,0:T(4,128)(2,1)} %copy.57) | data formatting | bytes 2359296 | tf_op jit(solution)/shard_map/while/body/eval_jaxpr/stack | solution.py:26
  28.5 4.1 %stack.22 = bf16[1,4,64,2304]{3,2,1,0:T(8,128)(2,1)} reshape(bf16[1,4,64,2,3,384]{5,4,3,2,1,0:T(4,128)(2,1)} %copy.58) | data formatting | bytes 2359296 | tf_op jit(solution)/shard_map/while/body/eval_jaxpr/stack | solution.py:26
  32.6 4.0 %fusion.32 = f32[4,4,64,2,64]{2,4,0,1,3:T(8,128)} fusion(bf16[1,4,64,2304]{3,2,1,0:T(8,128)(2,1)S(1)} %copy-done, bf16[1,4,64,2304]{3,2,1,0:T(8,128)(2,1)} %stack.22, bf16[4,64,2304]{2,1,0:T(8,128)(2,1)} %get-tuple-element.160), kind=kOutput, calls=%fused_computation.15.clone.1 | convolution fusion | flops 608698368 | bytes 4063232 | tf_op jit(solution)/shard_map/while/body/eval_jaxpr/ark,cbjk->abrcj/dot_general | solution.py:59
  44.7 4.0 %stack.21 = bf16[1,4,64,2304]{3,2,1,0:T(8,128)(2,1)} reshape(bf16[1,4,64,2,3,384]{5,4,3,2,1,0:T(4,128)(2,1)} %copy.57) | data formatting | bytes 2359296 | tf_op jit(solution)/shard_map/while/body/eval_jaxpr/stack | solution.py:26
  50.4 4.1 %stack.22 = bf16[1,4,64,2304]{3,2,1,0:T(8,128)(2,1)} reshape(bf16[1,4,64,2,3,384]{5,4,3,2,1,0:T(4,128)(2,1)} %copy.58) | data formatting | bytes 2359296 | tf_op jit(solution)/shard_map/while/body/eval_jaxpr/stack | solution.py:26
  54.5 4.0 %fusion.32 = f32[4,4,64,2,64]{2,4,0,1,3:T(8,128)} fusion(bf16[1,4,64,2304]{3,2,1,0:T(8,128)(2,1)S(1)} %copy-done, bf16[1,4,64,2304]{3,2,1,0:T(8,128)(2,1)} %stack.22, bf16[4,64,2304]{2,1,0:T(8,128)(2,1)} %get-tuple-element.160), kind=kOutput, calls=%fused_computation.15.clone.1 | convolution fusion | flops 608698368 | bytes 4063232 | tf_op jit(solution)/shard_map/while/body/eval_jaxpr/ark,cbjk->abrcj/dot_general | solution.py:59
  66.5 4.0 %stack.21 = bf16[1,4,64,2304]{3,2,1,0:T(8,128)(2,1)} reshape(bf16[1,4,64,2,3,384]{5,4,3,2,1,0:T(4,128)(2,1)} %copy.57) | data formatting | bytes 2359296 | tf_op jit(solution)/shard_map/while/body/eval_jaxpr/stack | solution.py:26
  72.2 4.1 %stack.22 = bf16[1,4,64,2304]{3,2,1,0:T(8,128)(2,1)} reshape(bf16[1,4,64,2,3,384]{5,4,3,2,1,0:T(4,128)(2,1)} %copy.58) | data formatting | bytes 2359296 | tf_op jit(solution)/shard_map/while/body/eval_jaxpr/stack | solution.py:26
  76.3 4.0 %fusion.32 = f32[4,4,64,2,64]{2,4,0,1,3:T(8,128)} fusion(bf16[1,4,64,2304]{3,2,1,0:T(8,128)(2,1)S(1)} %copy-done, bf16[1,4,64,2304]{3,2,1,0:T(8,128)(2,1)} %stack.22, bf16[4,64,2304]{2,1,0:T(8,128)(2,1)} %get-tuple-element.160), kind=kOutput, calls=%fused_computation.15.clone.1 | convolution fusion | flops 608698368 | bytes 4063232 | tf_op jit(solution)/shard_map/while/body/eval_jaxpr/ark,cbjk->abrcj/dot_general | solution.py:59
  94.1 4.1 %stack.22 = bf16[1,4,64,2304]{3,2,1,0:T(8,128)(2,1)} reshape(bf16[1,4,64,2,3,384]{5,4,3,2,1,0:T(4,128)(2,1)} %copy.58) | data formatting | bytes 2359296 | tf_op jit(solution)/shard_map/while/body/eval_jaxpr/stack | solution.py:26
  98.2 4.0 %fusion.32 = f32[4,4,64,2,64]{2,4,0,1,3:T(8,128)} fusion(bf16[1,4,64,2304]{3,2,1,0:T(8,128)(2,1)S(1)} %copy-done, bf16[1,4,64,2304]{3,2,1,0:T(8,128)(2,1)} %stack.22, bf16[4,64,2304]{2,1,0:T(8,128)(2,1)} %get-tuple-element.160), kind=kOutput, calls=%fused_computation.15.clone.1 | convolution fusion | flops 608698368 | bytes 4063232 | tf_op jit(solution)/shard_map/while/body/eval_jaxpr/ark,cbjk->abrcj/dot_general | solution.py:59
  110.2 4.0 %stack.21 = bf16[1,4,64,2304]{3,2,1,0:T(8,128)(2,1)} reshape(bf16[1,4,64,2,3,384]{5,4,3,2,1,0:T(4,128)(2,1)} %copy.57) | data formatting | bytes 2359296 | tf_op jit(solution)/shard_map/while/body/eval_jaxpr/stack | solution.py:26
  115.9 4.1 %stack.22 = bf16[1,4,64,2304]{3,2,1,0:T(8,128)(2,1)} reshape(bf16[1,4,64,2,3,384]{5,4,3,2,1,0:T(4,128)(2,1)} %copy.58) | data formatting | bytes 2359296 | tf_op jit(solution)/shard_map/while/body/eval_jaxpr/stack | solution.py:26
  120.0 4.0 %fusion.32 = f32[4,4,64,2,64]{2,4,0,1,3:T(8,128)} fusion(bf16[1,4,64,2304]{3,2,1,0:T(8,128)(2,1)S(1)} %copy-done, bf16[1,4,64,2304]{3,2,1,0:T(8,128)(2,1)} %stack.22, bf16[4,64,2304]{2,1,0:T(8,128)(2,1)} %get-tuple-element.160), kind=kOutput, calls=%fused_computation.15.clone.1 | convolution fusion | flops 608698368 | bytes 4063232 | tf_op jit(solution)/shard_map/while/body/eval_jaxpr/ark,cbjk->abrcj/dot_general | solution.py:59
  137.7 4.1 %stack.22 = bf16[1,4,64,2304]{3,2,1,0:T(8,128)(2,1)} reshape(bf16[1,4,64,2,3,384]{5,4,3,2,1,0:T(4,128)(2,1)} %copy.58) | data formatting | bytes 2359296 | tf_op jit(solution)/shard_map/while/body/eval_jaxpr/stack | solution.py:26
  141.9 4.0 %fusion.32 = f32[4,4,64,2,64]{2,4,0,1,3:T(8,128)} fusion(bf16[1,4,64,2304]{3,2,1,0:T(8,128)(2,1)S(1)} %copy-done, bf16[1,4,64,2304]{3,2,1,0:T(8,128)(2,1)} %stack.22, bf16[4,64,2304]{2,1,0:T(8,128)(2,1)} %get-tuple-element.160), kind=kOutput, calls=%fused_computation.15.clone.1 | convolution fusion | flops 608698368 | bytes 4063232 | tf_op jit(solution)/shard_map/while/body/eval_jaxpr/ark,cbjk->abrcj/dot_general | solution.py:59
  153.9 4.0 %stack.21 = bf16[1,4,64,2304]{3,2,1,0:T(8,128)(2,1)} reshape(bf16[1,4,64,2,3,384]{5,4,3,2,1,0:T(4,128)(2,1)} %copy.57) | data formatting | bytes 2359296 | tf_op jit(solution)/shard_map/while/body/eval_jaxpr/stack | solution.py:26
  159.6 4.1 %stack.22 = bf16[1,4,64,2304]{3,2,1,0:T(8,128)(2,1)} reshape(bf16[1,4,64,2,3,384]{5,4,3,2,1,0:T(4,128)(2,1)} %copy.58) | data formatting | bytes 2359296 | tf_op jit(solution)/shard_map/while/body/eval_jaxpr/stack | solution.py:26
  163.7 4.0 %fusion.32 = f32[4,4,64,2,64]{2,4,0,1,3:T(8,128)} fusion(bf16[1,4,64,2304]{3,2,1,0:T(8,128)(2,1)S(1)} %copy-done, bf16[1,4,64,2304]{3,2,1,0:T(8,128)(2,1)} %stack.22, bf16[4,64,2304]{2,1,0:T(8,128)(2,1)} %get-tuple-element.160), kind=kOutput, calls=%fused_computation.15.clone.1 | convolution fusion | flops 608698368 | bytes 4063232 | tf_op jit(solution)/shard_map/while/body/eval_jaxpr/ark,cbjk->abrcj/dot_general | solution.py:59
  181.4 4.1 %stack.22 = bf16[1,4,64,2304]{3,2,1,0:T(8,128)(2,1)} reshape(bf16[1,4,64,2,3,384]{5,4,3,2,1,0:T(4,128)(2,1)} %copy.58) | data formatting | bytes 2359296 | tf_op jit(solution)/shard_map/while/body/eval_jaxpr/stack | solution.py:26
  185.6 4.0 %fusion.32 = f32[4,4,64,2,64]{2,4,0,1,3:T(8,128)} fusion(bf16[1,4,64,2304]{3,2,1,0:T(8,128)(2,1)S(1)} %copy-done, bf16[1,4,64,2304]{3,2,1,0:T(8,128)(2,1)} %stack.22, bf16[4,64,2304]{2,1,0:T(8,128)(2,1)} %get-tuple-element.160), kind=kOutput, calls=%fused_computation.15.clone.1 | convolution fusion | flops 608698368 | bytes 4063232 | tf_op jit(solution)/shard_map/while/body/eval_jaxpr/ark,cbjk->abrcj/dot_general | solution.py:59
  194.5 156.0 %all-reduce.3.cloned.1.call-done = f32[8,16,64,128]{3,2,1,0:T(8,128)} async-done(((f32[8,16,64,128]{3,2,1,0:T(8,128)}), f32[8,16,64,128]{3,2,1,0:T(8,128)}) %all-reduce.3.cloned.1.call-update) | async-done | bytes 4194320
  359.1 9.5 %psum.7 = f32[256]{0:T(256)S(1)} all-reduce(f32[256]{0:T(256)S(1)} %multiply_reduce_fusion), channel_id=1, replica_groups=mesh['ta'=8,'sa'=4] {'sa'}, use_global_device_ids=true, to_apply=%region_4.5 | all-reduce | flops 256 | bytes 2048 | tf_op jit(solution)/shard_map/psum | solution.py:32
  (124 shorter events, 115.9 us)
Async XLA Ops:
  7.2 343.3 %all-reduce.3.cloned.1.call-start = ((), (), s32[]{:S(2)}) async-start(), calls=%async_computation.1 | async-start | bytes 8388608
  14.1 1.3 copy-start.2
  16.6 1.0 copy-start.3
  28.5 4.1 %copy-start = (bf16[1,4,64,2304]{3,2,1,0:T(8,128)(2,1)S(1)}, bf16[1,4,64,2304]{3,2,1,0:T(8,128)(2,1)}, u32[]{:S(2)}) copy-start(bf16[1,4,64,2304]{3,2,1,0:T(8,128)(2,1)} %stack.21) | copy-start | bytes 3538948 | tf_op jit(solution)/shard_map/while
  50.4 4.1 %copy-start = (bf16[1,4,64,2304]{3,2,1,0:T(8,128)(2,1)S(1)}, bf16[1,4,64,2304]{3,2,1,0:T(8,128)(2,1)}, u32[]{:S(2)}) copy-start(bf16[1,4,64,2304]{3,2,1,0:T(8,128)(2,1)} %stack.21) | copy-start | bytes 3538948 | tf_op jit(solution)/shard_map/while
  72.2 4.1 %copy-start = (bf16[1,4,64,2304]{3,2,1,0:T(8,128)(2,1)S(1)}, bf16[1,4,64,2304]{3,2,1,0:T(8,128)(2,1)}, u32[]{:S(2)}) copy-start(bf16[1,4,64,2304]{3,2,1,0:T(8,128)(2,1)} %stack.21) | copy-start | bytes 3538948 | tf_op jit(solution)/shard_map/while
  94.1 4.1 %copy-start = (bf16[1,4,64,2304]{3,2,1,0:T(8,128)(2,1)S(1)}, bf16[1,4,64,2304]{3,2,1,0:T(8,128)(2,1)}, u32[]{:S(2)}) copy-start(bf16[1,4,64,2304]{3,2,1,0:T(8,128)(2,1)} %stack.21) | copy-start | bytes 3538948 | tf_op jit(solution)/shard_map/while
  115.9 4.1 %copy-start = (bf16[1,4,64,2304]{3,2,1,0:T(8,128)(2,1)S(1)}, bf16[1,4,64,2304]{3,2,1,0:T(8,128)(2,1)}, u32[]{:S(2)}) copy-start(bf16[1,4,64,2304]{3,2,1,0:T(8,128)(2,1)} %stack.21) | copy-start | bytes 3538948 | tf_op jit(solution)/shard_map/while
  137.7 4.1 %copy-start = (bf16[1,4,64,2304]{3,2,1,0:T(8,128)(2,1)S(1)}, bf16[1,4,64,2304]{3,2,1,0:T(8,128)(2,1)}, u32[]{:S(2)}) copy-start(bf16[1,4,64,2304]{3,2,1,0:T(8,128)(2,1)} %stack.21) | copy-start | bytes 3538948 | tf_op jit(solution)/shard_map/while
  159.6 4.1 %copy-start = (bf16[1,4,64,2304]{3,2,1,0:T(8,128)(2,1)S(1)}, bf16[1,4,64,2304]{3,2,1,0:T(8,128)(2,1)}, u32[]{:S(2)}) copy-start(bf16[1,4,64,2304]{3,2,1,0:T(8,128)(2,1)} %stack.21) | copy-start | bytes 3538948 | tf_op jit(solution)/shard_map/while
  181.4 4.1 %copy-start = (bf16[1,4,64,2304]{3,2,1,0:T(8,128)(2,1)S(1)}, bf16[1,4,64,2304]{3,2,1,0:T(8,128)(2,1)}, u32[]{:S(2)}) copy-start(bf16[1,4,64,2304]{3,2,1,0:T(8,128)(2,1)} %stack.21) | copy-start | bytes 3538948 | tf_op jit(solution)/shard_map/while
  192.6 0.7 copy-start.4
  353.4 3.9 %copy-start.1 = (bf16[1,256,2,3,1,384]{5,2,4,3,1,0:T(2,128)(2,1)S(1)}, bf16[1,256,2,3,1,384]{5,2,4,3,1,0:T(2,128)(2,1)}, u32[]{:S(2)}) copy-start(bf16[1,256,2,3,1,384]{5,2,4,3,1,0:T(2,128)(2,1)} %param.5) | copy-start | bytes 3538948
  353.4 19.2 %all-to-all-start = ((f32[8,4,64,1,128]{4,1,0,3,2:T(4,128)}), f32[8,4,64,1,128]{4,1,0,3,2:T(4,128)S(1)}, u32[]{:S(2)}, u32[]{:S(2)}) async-start(f32[8,4,64,1,128]{4,1,0,3,2:T(4,128)} %copy.41), calls=%async_computation | async-start | bytes 2097152 | tf_op jit(solution)/shard_map/all_to_all | solution.py:67
Sparse Core Ops, SparseCore 0:
  192.7 157.6 all-reduce.2
where the time goes:
time: 383 us; the launch traced here: 381 us
  waiting for transfers between devices  159 us (42%)
  local copies, waits for them, and re-layouts  129 us (34%)
  other arithmetic  32.5 us (8%)
  matrix products  31.9 us (8%)
  between operations  14.8 us (4%)
  blocking collectives  9.53 us (2%)
  starting transfers between devices  3.91 us (1%)
    unnamed x2, waiting for transfers between devices  156 us
    another operation x16, local copies, waits for them, and re-layouts, phased_right(): right_cols = jnp.stack([first_half, second_half], axis=1)  64.6 us
    dot_general x8, matrix products, one_momentum(): jnp.einsum('ark,cbjk->abrcj', left_rows, right_cols, preferred_element_ty...  31.9 us
    another operation x8, other arithmetic, phased_right(): first_half = jnp.stack([phased_re, phased_im], axis=3)  14.5 us
    another operation x8, local copies, waits for them, and re-layouts, phased_right(): second_half = jnp.stack([phased_im, -phased_re], axis=3)  13.9 us
    another operation x8, local copies, waits for them, and re-layouts, phased_right(): first_half = jnp.stack([phased_re, phased_im], axis=3)  13.9 us
    transpose x8, local copies, waits for them, and re-layouts, one_momentum(): jnp.einsum('ark,cbjk->abrcj', left_rows, right_cols, preferred_element_ty...  12.7 us
    psum x1, blocking collectives, spatial_norms(): summed = lax.psum(local_sums, 'sa')  9.53 us
  transfers between devices with their start and end apart: 2, of which 2 were waited for; matrix products, arithmetic and copies ran while one was open for 1% of the time, Pallas kernels for 0%

commit v1 on v0

v1 whole, which is shorter than its diff:
```python
import functools
import math

import jax
import jax.numpy as jnp
from jax import lax
from jax.experimental import pallas as pl
from jax.experimental.pallas import tpu as pltpu
from jax.sharding import PartitionSpec as P

NC = 3
BS = 64
NBLK = 4
LX = 96
MESH = pl.DeviceIdType.MESH

full_turn = 2.0 * math.pi


def kernel(
    n, nta, scale, inv_count,
    order_ref, cos_ref, sin_ref, ev_ref,
    out_ref, norm_ref,
    left, right, parts, rbuf, lbuf, final, recv, nbuf,
    rsend, rrecv, lsend, lrecv, asend, arecv, nsend, nrecv,
):
    t, z = lax.axis_index("ta"), lax.axis_index("sa")
    moms, planes = cos_ref.shape
    ppd = NBLK * NBLK // n
    rows = BS // nta
    half = NC * planes

    barrier = pltpu.get_barrier_semaphore()
    for j in range(1, n):
        pl.semaphore_signal(barrier, inc=1, device_id={"sa": lax.rem(z + j, n)}, device_id_type=MESH)
    for j in range(1, nta):
        pl.semaphore_signal(barrier, inc=1, device_id={"ta": lax.rem(t + j, nta)}, device_id_type=MESH)

    for b in range(NBLK):
        stored = order_ref[b]
        for k in range(2 * NC):
            left[b * BS:(b + 1) * BS, k * planes:(k + 1) * planes] = ev_ref[stored, k]
    squares = []
    for b in range(NBLK):
        total = jnp.zeros((BS, 128), jnp.float32)
        for k in range(2 * NC):
            for lane in range(0, planes, 128):
                value = ev_ref[b, k, :, lane:lane + 128].astype(jnp.float32)
                total = total + value * value
        squares.append(total)
    nbuf[z] = lax.dot_general(
        jnp.ones((8, 128), jnp.float32), jnp.concatenate(squares, axis=0), (((1,), (1,)), ((), ())),
        precision=lax.Precision.HIGHEST, preferred_element_type=jnp.float32,
    )

    pl.semaphore_wait(barrier, n - 1 + nta - 1)

    def norm_copy(peer, slot):
        return pltpu.make_async_remote_copy(
            src_ref=nbuf.at[slot], dst_ref=nbuf.at[slot], send_sem=nsend.at[peer], recv_sem=nrecv.at[slot],
            device_id={"sa": peer}, device_id_type=MESH,
        )

    for j in range(1, n):
        norm_copy(lax.rem(z + j, n), z).start()

    def shard(ref, p, s):
        return ref.at[p, pl.ds(s * ppd, ppd)]

    def rightward(src, p, s):
        return pltpu.make_async_remote_copy(
            src_ref=shard(src, p, s), dst_ref=shard(rbuf, p, s), send_sem=rsend.at[p, s], recv_sem=rrecv.at[p, s],
            device_id={"sa": lax.rem(z + 1, n)}, device_id_type=MESH,
        )

    def leftward(src, p, s):
        return pltpu.make_async_remote_copy(
            src_ref=shard(src, p, s), dst_ref=shard(lbuf, p, s), send_sem=lsend.at[p, s], recv_sem=lrecv.at[p, s],
            device_id={"sa": lax.rem(z + n - 1, n)}, device_id_type=MESH,
        )

    def compute(p, carry):
        for c in range(NC):
            lanes = slice(c * planes, (c + 1) * planes)
            upper = slice(half + c * planes, half + (c + 1) * planes)
            cosine = cos_ref[pl.ds(p, 1), :]
            sine = sin_ref[pl.ds(p, 1), :]
            for b in range(NBLK):
                re = left[b * BS:(b + 1) * BS, lanes].astype(jnp.float32)
                im = left[b * BS:(b + 1) * BS, upper].astype(jnp.float32)
                phased_re = (re * cosine + im * sine).astype(jnp.bfloat16)
                phased_im = (im * cosine - re * sine).astype(jnp.bfloat16)
                first = slice(2 * b * BS, (2 * b + 1) * BS)
                second = slice((2 * b + 1) * BS, (2 * b + 2) * BS)
                right[first, lanes] = phased_re
                right[first, upper] = phased_im
                right[second, lanes] = phased_im
                right[second, upper] = -phased_re
        for pair in range(NBLK // 2):
            product = lax.dot_general(
                left[...], right[pair * 4 * BS:(pair + 1) * 4 * BS, :], (((1,), (1,)), ((), ())),
                preferred_element_type=jnp.float32,
            )
            for a in range(NBLK):
                for b in range(2):
                    parts[p, a * NBLK + 2 * pair + b] = product[a * BS:(a + 1) * BS, b * 2 * BS:(b + 1) * 2 * BS]

        @pl.when(z == 0)
        def _():
            for s in range(n - 1, 0, -1):
                rightward(parts, p, s).start()

        @pl.when(z == n - 1)
        def _():
            for s in range(n - 1):
                leftward(parts, p, s).start()

        return carry

    lax.fori_loop(0, moms, compute, 0)

    def rows_copy(p, peer):
        return pltpu.make_async_remote_copy(
            src_ref=final.at[p, peer], dst_ref=recv.at[p, t], send_sem=asend.at[p], recv_sem=arecv.at[p],
            device_id={"ta": peer}, device_id_type=MESH,
        )

    last = jnp.maximum(z - 1, n - 2 - z)

    def step(i, carry):
        p_right = i - (z - 1)
        p_left = i - (n - 2 - z)
        p_final = i - last
        p_out = p_final - 1

        @pl.when((z > 0) & (p_right >= 0) & (p_right < moms))
        def _():
            for s in range(n - 1, 0, -1):
                @pl.when(s > z)
                def _():
                    copy = rightward(rbuf, p_right, s)
                    copy.wait_recv()
                    for k in range(ppd):
                        rbuf[p_right, s * ppd + k] += parts[p_right, s * ppd + k]
                    copy.start()

        @pl.when((z < n - 1) & (p_left >= 0) & (p_left < moms))
        def _():
            for s in range(n - 1):
                @pl.when(s < z)
                def _():
                    copy = leftward(lbuf, p_left, s)
                    copy.wait_recv()
                    for k in range(ppd):
                        lbuf[p_left, s * ppd + k] += parts[p_left, s * ppd + k]
                    copy.start()

        @pl.when((p_final >= 0) & (p_final < moms))
        def _():
            @pl.when(z > 0)
            def _():
                rightward(rbuf, p_final, z).wait_recv()
                for k in range(ppd):
                    parts[p_final, z * ppd + k] += rbuf[p_final, z * ppd + k]

            @pl.when(z < n - 1)
            def _():
                leftward(lbuf, p_final, z).wait_recv()
                for k in range(ppd):
                    parts[p_final, z * ppd + k] += lbuf[p_final, z * ppd + k]

            for k in range(ppd):
                value = parts[p_final, z * ppd + k] * scale
                for peer in range(nta):
                    final[p_final, peer, k] = value[peer * rows:(peer + 1) * rows]
            for j in range(1, nta):
                rows_copy(p_final, lax.rem(t + j, nta)).start()
            recv[p_final, t] = final[p_final, t]

        @pl.when((p_out >= 0) & (p_out < moms))
        def _():
            arrived = recv.at[p_out, pl.ds(0, nta - 1)]
            pltpu.make_async_copy(arrived, arrived, arecv.at[p_out]).wait()
            for source in range(nta):
                for k in range(ppd):
                    out_ref[p_out, k, :, source, :] = recv[p_out, source, k]

        return carry

    lax.fori_loop(0, moms + n - 1, step, 0)

    for j in range(1, n):
        norm_copy(lax.rem(z + j, n), lax.rem(z + j, n)).wait_recv()
    total = nbuf[0]
    for q in range(1, n):
        total = total + nbuf[q]
    norm_ref[...] = total[0:1] * inv_count
    for j in range(1, n):
        norm_copy(lax.rem(z + j, n), z).wait_send()

    def drain(p, carry):
        for s in range(n):
            @pl.when(s > z)
            def _():
                rightward(parts, p, s).wait_send()

            @pl.when(s < z)
            def _():
                leftward(parts, p, s).wait_send()
        sent = final.at[p, pl.ds(0, nta - 1)]
        pltpu.make_async_copy(sent, sent, asend.at[p]).wait()
        return carry

    lax.fori_loop(0, moms, drain, 0)


def body(eigenvectors, momenta, block_order):
    planes = eigenvectors.shape[-1]
    n, nta = lax.axis_size("sa"), lax.axis_size("ta")
    moms = momenta.shape[0]
    nv = eigenvectors.shape[1]
    ppd = NBLK * NBLK // n
    rows = BS // nta
    stored = eigenvectors.reshape(NBLK, BS, 2 * NC, planes).transpose(0, 2, 1, 3)
    site_index = jnp.arange(planes, dtype=jnp.int32)
    phase_index = (
        momenta[:, 0:1] * (site_index % LX)[None, :]
        + momenta[:, 1:2] * (site_index // LX)[None, :]
        + momenta[:, 2:3] * lax.axis_index("sa")
    )
    angles = jnp.mod(phase_index, LX).astype(jnp.float32) * (full_turn / LX)
    count = 2 * NC * n * planes
    f32 = jnp.float32
    vmem = pl.BlockSpec(memory_space=pltpu.VMEM)
    dma = pltpu.SemaphoreType.DMA
    fields, norms = pl.pallas_call(
        functools.partial(kernel, n, nta, 1.0 / math.sqrt(count), 1.0 / count),
        out_shape=(
            jax.ShapeDtypeStruct((moms, ppd, rows, nta, 2 * BS), f32),
            jax.ShapeDtypeStruct((1, nv), f32),
        ),
        in_specs=[pl.BlockSpec(memory_space=pltpu.SMEM), vmem, vmem, vmem],
        out_specs=(vmem, vmem),
        scratch_shapes=[
            pltpu.VMEM((nv, 2 * NC * planes), jnp.bfloat16),
            pltpu.VMEM((2 * nv, 2 * NC * planes), jnp.bfloat16),
            pltpu.VMEM((moms, NBLK * NBLK, BS, 2 * BS), f32),
            pltpu.VMEM((moms, NBLK * NBLK, BS, 2 * BS), f32),
            pltpu.VMEM((moms, NBLK * NBLK, BS, 2 * BS), f32),
            pltpu.VMEM((moms, nta, ppd, rows, 2 * BS), f32),
            pltpu.VMEM((moms, nta, ppd, rows, 2 * BS), f32),
            pltpu.VMEM((n, 8, nv), f32),
            dma((moms, n)), dma((moms, n)), dma((moms, n)), dma((moms, n)),
            dma((moms,)), dma((moms,)), dma((n,)), dma((n,)),
        ],
        compiler_params=pltpu.CompilerParams(collective_id=0, has_side_effects=True),
    )(block_order, jnp.cos(angles), jnp.sin(angles), stored)
    return fields, norms


def solution(mesh):
    return jax.shard_map(
        body,
        mesh=mesh,
        in_specs=(P("ta", None, None, None, "sa", None), P(), P()),
        out_specs=(P(None, "sa", "ta", None, None), P("ta", None)),
        check_vma=False,
    )
```

time: 383 us -> 95.1 us (0.25)
  waiting for transfers between devices: 159 us -> 0 us
  local copies, waits for them, and re-layouts: 129 us -> 5.44 us
  Pallas kernels: 0 us -> 87.2 us
  matrix products: 31.9 us -> 0 us
  other arithmetic: 32.5 us -> 1.55 us
  between operations: 14.8 us -> 0.66 us
  blocking collectives: 9.53 us -> 0 us
  starting transfers between devices: 3.91 us -> 0 us
    unnamed x2 -> x0, waiting for transfers between devices: 156 us -> none
    another operation x32 -> x0, local copies, waits for them, and re-layouts: 92.4 us -> none  [the longest x16 64.6 us: phased_right(): right_cols = jnp.stack([first_half, second_half], axis=1)]
    pallas_call x0 -> x1, Pallas kernels: none -> 87.2 us  [body(): pl.pallas_call(functools.partial(kernel, n, nta, 1.0 / math.sqrt(count),...]
    dot_general x8 -> x0, matrix products: 31.9 us -> none  [one_momentum(): jnp.einsum('ark,cbjk->abrcj', left_rows, right_cols, preferred_element_ty...]
    another operation x8 -> x0, other arithmetic: 14.5 us -> none  [phased_right(): first_half = jnp.stack([phased_re, phased_im], axis=3)]
    transpose x8 -> x0, local copies, waits for them, and re-layouts: 12.7 us -> none  [one_momentum(): jnp.einsum('ark,cbjk->abrcj', left_rows, right_cols, preferred_element_ty...]
    psum x1 -> x0, blocking collectives: 9.53 us -> none  [spatial_norms(): summed = lax.psum(local_sums, 'sa')]
    dynamic_update_slice x8 -> x0, local copies, waits for them, and re-layouts: 6.7 us -> none  [body(): fields = lax.map(one_momentum, (cosines[:, None, :], sine_vals[:, None, :]))]
  transfers between devices with their start and end apart: 2 -> 0, of which waited for: 2 -> 0; matrix products, arithmetic and copies ran while one was open for 1% -> 0% of each run, Pallas kernels for 0% -> 0%
where the time goes in v1:
time: 95.1 us; the launch traced here: 94.9 us
  Pallas kernels  87.2 us (92%)
  local copies, waits for them, and re-layouts  5.44 us (6%)
  other arithmetic  1.55 us (2%)
    pallas_call x1, Pallas kernels, body(): pl.pallas_call(functools.partial(kernel, n, nta, 1.0 / math.sqrt(count),...  87.2 us
    unnamed x5, local copies, waits for them, and re-layouts  4.29 us

profile of v1, /device:TPU:0, one launch (start us, length us, event | category | flops | bytes accessed | tf_op | source)
XLA Modules:
  0.0 94.9 jit_solution(5105781132064423156)
XLA Ops:
  0.6 0.8 slice_bitcast_fusion.1
  1.4 0.7 fusion.5
  2.2 1.4 %copy.5 = bf16[1,256,2,3,1,384]{5,1,3,2,4,0:T(8,128)(2,1)S(1)} copy(bf16[1,256,2,3,1,384]{5,2,4,3,1,0:T(2,128)(2,1)} %param.3) | data formatting | bytes 2359296 | tf_op args[0]
  3.6 1.1 %copy.8 = bf16[4,64,6,384]{3,1,2,0:T(8,128)(2,1)} copy(bf16[4,64,6,384]{3,1,0,2:T(8,128)(2,1)S(1)} %bitcast.11) | data formatting | bytes 2359296 | tf_op jit(solution)/shard_map/reshape | solution.py:224
  4.8 87.2 %shard_map.50 = (f32[8,4,8,8,128]{4,3,2,1,0:T(8,128)}, f32[1,256]{1,0:T(1,128)}) custom-call(s32[4]{0:T(128)} %order_ref.1, f32[8,384]{1,0:T(8,128)} %get-tuple-element.3.cos_ref, f32[8,384]{1,0:T(8,128)} %get-tuple-element.2.sin_ref, bf16[4,6,64,384]{3,2,1,0:T(8,128)(2,1)} %bitcast.10), custom_call_target="tpu_custom_call" | custom-call | tf_op jit(solution)/shard_map/pallas_call | solution.py:236
  92.0 0.0 copy-start
  92.0 2.3 %copy.11 = f32[8,4,8,8,128]{4,3,2,1,0:T(8,128)} copy(f32[8,4,8,8,128]{4,3,2,1,0:T(8,128)} %get-tuple-element.11) | data formatting | bytes 2097152
  94.3 0.0 copy-done
  94.3 0.6 copy.12
  (1 shorter events, 0.0 us)
Async XLA Ops:
  92.0 2.3 %copy-start = (f32[1,256]{1,0:T(1,128)S(1)}, f32[1,256]{1,0:T(1,128)}, u32[]{:S(2)}) copy-start(f32[1,256]{1,0:T(1,128)} %get-tuple-element.12) | copy-start | bytes 3076

commit v2 on v1

--- a/solution.py
+++ b/solution.py
@@ -19,13 +19,13 @@
 
 def kernel(
     n, nta, scale, inv_count,
-    order_ref, cos_ref, sin_ref, ev_ref,
+    order_ref, momenta_ref, ev_ref,
     out_ref, norm_ref,
     left, right, parts, rbuf, lbuf, final, recv, nbuf,
     rsend, rrecv, lsend, lrecv, asend, arecv, nsend, nrecv,
 ):
     t, z = lax.axis_index("ta"), lax.axis_index("sa")
-    moms, planes = cos_ref.shape
+    moms, planes = momenta_ref.shape[1], ev_ref.shape[-1]
     ppd = NBLK * NBLK // n
     rows = BS // nta
     half = NC * planes
@@ -39,31 +39,13 @@
     for b in range(NBLK):
         stored = order_ref[b]
         for k in range(2 * NC):
-            left[b * BS:(b + 1) * BS, k * planes:(k + 1) * planes] = ev_ref[stored, k]
-    squares = []
-    for b in range(NBLK):
-        total = jnp.zeros((BS, 128), jnp.float32)
-        for k in range(2 * NC):
-            for lane in range(0, planes, 128):
-                value = ev_ref[b, k, :, lane:lane + 128].astype(jnp.float32)
-                total = total + value * value
-        squares.append(total)
-    nbuf[z] = lax.dot_general(
-        jnp.ones((8, 128), jnp.float32), jnp.concatenate(squares, axis=0), (((1,), (1,)), ((), ())),
-        precision=lax.Precision.HIGHEST, preferred_element_type=jnp.float32,
-    )
-
-    pl.semaphore_wait(barrier, n - 1 + nta - 1)
-
+            left[b * BS:(b + 1) * BS, k * planes:(k + 1) * planes] = ev_ref[k, stored]
     def norm_copy(peer, slot):
         return pltpu.make_async_remote_copy(
             src_ref=nbuf.at[slot], dst_ref=nbuf.at[slot], send_sem=nsend.at[peer], recv_sem=nrecv.at[slot],
             device_id={"sa": peer}, device_id_type=MESH,
         )
 
-    for j in range(1, n):
-        norm_copy(lax.rem(z + j, n), z).start()
-
     def shard(ref, p, s):
         return ref.at[p, pl.ds(s * ppd, ppd)]
 
@@ -79,12 +61,18 @@
             device_id={"sa": lax.rem(z + n - 1, n)}, device_id_type=MESH,
         )
 
-    def compute(p, carry):
+    def compute(p):
+        site = lax.broadcasted_iota(jnp.int32, (1, planes), 1)
+        phase_index = (
+            momenta_ref[0, p] * lax.rem(site, LX)
+            + momenta_ref[1, p] * lax.div(site, LX)
+            + momenta_ref[2, p] * z
+        )
+        angles = jnp.mod(phase_index, LX).astype(jnp.float32) * (full_turn / LX)
+        cosine, sine = jnp.cos(angles), jnp.sin(angles)
         for c in range(NC):
             lanes = slice(c * planes, (c + 1) * planes)
             upper = slice(half + c * planes, half + (c + 1) * planes)
-            cosine = cos_ref[pl.ds(p, 1), :]
-            sine = sin_ref[pl.ds(p, 1), :]
             for b in range(NBLK):
                 re = left[b * BS:(b + 1) * BS, lanes].astype(jnp.float32)
                 im = left[b * BS:(b + 1) * BS, upper].astype(jnp.float32)
@@ -105,6 +93,7 @@
                 for b in range(2):
                     parts[p, a * NBLK + 2 * pair + b] = product[a * BS:(a + 1) * BS, b * 2 * BS:(b + 1) * 2 * BS]
 
+    def open_lines(p):
         @pl.when(z == 0)
         def _():
             for s in range(n - 1, 0, -1):
@@ -115,9 +104,31 @@
             for s in range(n - 1):
                 leftward(parts, p, s).start()
 
+    def compute_and_open(p, carry):
+        compute(p)
+        open_lines(p)
         return carry
 
-    lax.fori_loop(0, moms, compute, 0)
+    compute(0)
+    pl.semaphore_wait(barrier, n - 1 + nta - 1)
+    open_lines(0)
+    lax.fori_loop(1, moms, compute_and_open, 0)
+
+    squares = []
+    for b in range(NBLK):
+        total = jnp.zeros((BS, 128), jnp.float32)
+        for k in range(2 * NC):
+            for lane in range(0, planes, 128):
+                value = ev_ref[k, b, :, lane:lane + 128].astype(jnp.float32)
+                total = total + value * value
+        squares.append(total)
+    nbuf[z] = lax.dot_general(
+        jnp.ones((8, 128), jnp.float32), jnp.concatenate(squares, axis=0), (((1,), (1,)), ((), ())),
+        precision=lax.Precision.HIGHEST, preferred_element_type=jnp.float32,
+    )
+
+    for j in range(1, n):
+        norm_copy(lax.rem(z + j, n), z).start()
 
     def rows_copy(p, peer):
         return pltpu.make_async_remote_copy(
@@ -221,17 +232,11 @@
     nv = eigenvectors.shape[1]
     ppd = NBLK * NBLK // n
     rows = BS // nta
-    stored = eigenvectors.reshape(NBLK, BS, 2 * NC, planes).transpose(0, 2, 1, 3)
-    site_index = jnp.arange(planes, dtype=jnp.int32)
-    phase_index = (
-        momenta[:, 0:1] * (site_index % LX)[None, :]
-        + momenta[:, 1:2] * (site_index // LX)[None, :]
-        + momenta[:, 2:3] * lax.axis_index("sa")
-    )
-    angles = jnp.mod(phase_index, LX).astype(jnp.float32) * (full_turn / LX)
+    stored = eigenvectors.reshape(NBLK, BS, 2 * NC, planes).transpose(2, 0, 1, 3)
     count = 2 * NC * n * planes
     f32 = jnp.float32
     vmem = pl.BlockSpec(memory_space=pltpu.VMEM)
+    smem = pl.BlockSpec(memory_space=pltpu.SMEM)
     dma = pltpu.SemaphoreType.DMA
     fields, norms = pl.pallas_call(
         functools.partial(kernel, n, nta, 1.0 / math.sqrt(count), 1.0 / count),
@@ -239,7 +244,7 @@
             jax.ShapeDtypeStruct((moms, ppd, rows, nta, 2 * BS), f32),
             jax.ShapeDtypeStruct((1, nv), f32),
         ),
-        in_specs=[pl.BlockSpec(memory_space=pltpu.SMEM), vmem, vmem, vmem],
+        in_specs=[smem, smem, vmem],
         out_specs=(vmem, vmem),
         scratch_shapes=[
             pltpu.VMEM((nv, 2 * NC * planes), jnp.bfloat16),
@@ -253,8 +258,8 @@
             dma((moms, n)), dma((moms, n)), dma((moms, n)), dma((moms, n)),
             dma((moms,)), dma((moms,)), dma((n,)), dma((n,)),
         ],
-        compiler_params=pltpu.CompilerParams(collective_id=0, has_side_effects=True),
-    )(block_order, jnp.cos(angles), jnp.sin(angles), stored)
+        compiler_params=pltpu.CompilerParams(collective_id=0, has_side_effects=True, vmem_limit_bytes=30 * 1024 * 1024),
+    )(block_order, momenta.T, stored)
     return fields, norms
 
 

time: 95.1 us -> 88 us (0.925)
  Pallas kernels: 87.2 us -> 84.2 us
  local copies, waits for them, and re-layouts: 5.44 us -> 2.98 us
  other arithmetic: 1.55 us -> 0 us
    pallas_call x1, Pallas kernels: 87.2 us -> 84.2 us  [body(): pl.pallas_call(functools.partial(kernel, n, nta, 1.0 / math.sqrt(count),...]
    unnamed x5 -> x7, local copies, waits for them, and re-layouts: 4.29 us -> 2.98 us
    reshape x1 -> x0, local copies, waits for them, and re-layouts: 1.15 us -> none  [body(): eigenvectors.reshape(NBLK, BS, 2 * NC, planes).transpose(0, 2, 1, 3)]
where the time goes in v2:
time: 88 us; the launch traced here: 87.8 us
  Pallas kernels  84.2 us (96%)
  local copies, waits for them, and re-layouts  2.98 us (3%)
    pallas_call x1, Pallas kernels, body(): pl.pallas_call(functools.partial(kernel, n, nta, 1.0 / math.sqrt(count),...  84.2 us
    unnamed x7, local copies, waits for them, and re-layouts  2.98 us

profile of v2, /device:TPU:0, one launch (start us, length us, event | category | flops | bytes accessed | tf_op | source)
XLA Modules:
  0.0 87.8 jit_solution(16356714151487061939)
XLA Ops:
  0.6 0.0 copy-start
  0.6 0.0 copy-start.1
  0.6 1.4 %copy.5 = bf16[1,256,2,3,1,384]{5,1,3,2,4,0:T(8,128)(2,1)S(1)} copy(bf16[1,256,2,3,1,384]{5,2,4,3,1,0:T(2,128)(2,1)} %param.3) | data formatting | bytes 2359296 | tf_op args[0]
  2.1 0.0 copy-done
  2.1 0.0 copy-done.1
  2.1 84.2 %shard_map.50 = (f32[8,4,8,8,128]{4,3,2,1,0:T(8,128)S(1)}, f32[1,256]{1,0:T(1,128)S(1)}) custom-call(s32[4]{0:T(128)S(1)} %copy-done.1, s32[3,8]{1,0:T(4,128)S(1)} %bitcast.5, bf16[6,4,64,384]{3,2,1,0:T(8,128)(2,1)S(1)} %bitcast.4), custom_call_target="tpu_custom_call" | custom-call | tf_op jit(solution)/shard_map/pallas_call | solution.py:241
  86.3 1.0 %copy.8 = f32[8,4,8,8,128]{4,3,2,1,0:T(8,128)} copy(f32[8,4,8,8,128]{4,3,2,1,0:T(8,128)S(1)} %get-tuple-element.4) | data formatting | bytes 2097152
  87.2 0.6 copy.9
Async XLA Ops:
  0.6 1.5 %copy-start = (s32[8,3]{0,1:T(4,128)S(1)}, s32[8,3]{0,1:T(4,128)}, u32[]{:S(2)}) copy-start(s32[8,3]{0,1:T(4,128)} %param.4) | copy-start | bytes 292
  0.6 1.5 %copy-start.1 = (s32[4]{0:T(128)S(1)}, s32[4]{0:T(128)}, u32[]{:S(2)}) copy-start(s32[4]{0:T(128)} %order_ref.1) | copy-start | bytes 52

commit v3 on v2

--- a/solution.py
+++ b/solution.py
@@ -93,26 +93,39 @@
                 for b in range(2):
                     parts[p, a * NBLK + 2 * pair + b] = product[a * BS:(a + 1) * BS, b * 2 * BS:(b + 1) * 2 * BS]
 
-    def open_lines(p):
+    def open_lines(slot):
         @pl.when(z == 0)
         def _():
             for s in range(n - 1, 0, -1):
-                rightward(parts, p, s).start()
+                p = slot - (n - 1 - s)
+
+                @pl.when((p >= 0) & (p < moms))
+                def _():
+                    rightward(parts, p, s).start()
 
         @pl.when(z == n - 1)
         def _():
             for s in range(n - 1):
-                leftward(parts, p, s).start()
+                p = slot - s
+
+                @pl.when((p >= 0) & (p < moms))
+                def _():
+                    leftward(parts, p, s).start()
 
     def compute_and_open(p, carry):
         compute(p)
         open_lines(p)
+        return carry
+
+    def only_open(slot, carry):
+        open_lines(slot)
         return carry
 
     compute(0)
     pl.semaphore_wait(barrier, n - 1 + nta - 1)
     open_lines(0)
     lax.fori_loop(1, moms, compute_and_open, 0)
+    lax.fori_loop(moms, moms + n - 2, only_open, 0)
 
     squares = []
     for b in range(NBLK):
@@ -136,35 +149,31 @@
             device_id={"ta": peer}, device_id_type=MESH,
         )
 
-    last = jnp.maximum(z - 1, n - 2 - z)
-
     def step(i, carry):
-        p_right = i - (z - 1)
-        p_left = i - (n - 2 - z)
-        p_final = i - last
+        p_final = i - (n - 2)
         p_out = p_final - 1
 
-        @pl.when((z > 0) & (p_right >= 0) & (p_right < moms))
-        def _():
-            for s in range(n - 1, 0, -1):
-                @pl.when(s > z)
-                def _():
-                    copy = rightward(rbuf, p_right, s)
-                    copy.wait_recv()
-                    for k in range(ppd):
-                        rbuf[p_right, s * ppd + k] += parts[p_right, s * ppd + k]
-                    copy.start()
-
-        @pl.when((z < n - 1) & (p_left >= 0) & (p_left < moms))
-        def _():
-            for s in range(n - 1):
-                @pl.when(s < z)
-                def _():
-                    copy = leftward(lbuf, p_left, s)
-                    copy.wait_recv()
-                    for k in range(ppd):
-                        lbuf[p_left, s * ppd + k] += parts[p_left, s * ppd + k]
-                    copy.start()
+        for s in range(n - 1, 0, -1):
+            p_right = i - (z - 1) - (n - 1 - s)
+
+            @pl.when((z > 0) & (s > z) & (p_right >= 0) & (p_right < moms))
+            def _():
+                copy = rightward(rbuf, p_right, s)
+                copy.wait_recv()
+                for k in range(ppd):
+                    rbuf[p_right, s * ppd + k] += parts[p_right, s * ppd + k]
+                copy.start()
+
+        for s in range(n - 1):
+            p_left = i - (n - 2 - z) - s
+
+            @pl.when((z < n - 1) & (s < z) & (p_left >= 0) & (p_left < moms))
+            def _():
+                copy = leftward(lbuf, p_left, s)
+                copy.wait_recv()
+                for k in range(ppd):
+                    lbuf[p_left, s * ppd + k] += parts[p_left, s * ppd + k]
+                copy.start()
 
         @pl.when((p_final >= 0) & (p_final < moms))
         def _():

time: 88 us -> 83.6 us (0.950)
  Pallas kernels: 84.2 us -> 79.8 us
    pallas_call x1, Pallas kernels: 84.2 us -> 79.8 us  [body(): pl.pallas_call(functools.partial(kernel, n, nta, 1.0 / math.sqrt(count),...]
where the time goes in v3:
time: 83.6 us; the launch traced here: 83.5 us
  Pallas kernels  79.8 us (95%)
  local copies, waits for them, and re-layouts  2.98 us (4%)
    pallas_call x1, Pallas kernels, body(): pl.pallas_call(functools.partial(kernel, n, nta, 1.0 / math.sqrt(count),...  79.8 us
    unnamed x7, local copies, waits for them, and re-layouts  2.98 us

profile of v3, /device:TPU:0, one launch (start us, length us, event | category | flops | bytes accessed | tf_op | source)
XLA Modules:
  0.0 83.5 jit_solution(15953533911063074427)
XLA Ops:
  0.6 0.0 copy-start
  0.6 0.0 copy-start.1
  0.6 1.4 %copy.5 = bf16[1,256,2,3,1,384]{5,1,3,2,4,0:T(8,128)(2,1)S(1)} copy(bf16[1,256,2,3,1,384]{5,2,4,3,1,0:T(2,128)(2,1)} %param.3) | data formatting | bytes 2359296 | tf_op args[0]
  2.1 0.0 copy-done
  2.1 0.0 copy-done.1
  2.1 79.8 %shard_map.50 = (f32[8,4,8,8,128]{4,3,2,1,0:T(8,128)S(1)}, f32[1,256]{1,0:T(1,128)S(1)}) custom-call(s32[4]{0:T(128)S(1)} %copy-done.1, s32[3,8]{1,0:T(4,128)S(1)} %bitcast.5, bf16[6,4,64,384]{3,2,1,0:T(8,128)(2,1)S(1)} %bitcast.4), custom_call_target="tpu_custom_call" | custom-call | tf_op jit(solution)/shard_map/pallas_call | solution.py:250
  81.9 1.0 %copy.8 = f32[8,4,8,8,128]{4,3,2,1,0:T(8,128)} copy(f32[8,4,8,8,128]{4,3,2,1,0:T(8,128)S(1)} %get-tuple-element.4) | data formatting | bytes 2097152
  82.9 0.6 copy.9
Async XLA Ops:
  0.6 1.5 %copy-start = (s32[8,3]{0,1:T(4,128)S(1)}, s32[8,3]{0,1:T(4,128)}, u32[]{:S(2)}) copy-start(s32[8,3]{0,1:T(4,128)} %param.4) | copy-start | bytes 292
  0.6 1.5 %copy-start.1 = (s32[4]{0:T(128)S(1)}, s32[4]{0:T(128)}, u32[]{:S(2)}) copy-start(s32[4]{0:T(128)} %order_ref.1) | copy-start | bytes 52
